TPU v7x, 32 devices: a whole 2x2x4 slice. The times are simulated.
32 devices in a mesh: rep: 8 (over y, x, core), tp: 4 (over z).
Axes of the slice: x: 2, y: 2, z: 4, core: 2. Of those that a mesh axis runs over, the one named last changes fastest.
Arguments:
- flat_buffer: bfloat16 [578912256], P(('rep', 'tp')), may hold values from -60 to 60
- shard_pad: int32 [2, 6], replicated, may hold values from 0 to 2
Outputs:
- q_served: bfloat16 [2, 6144, 6144], P(None, 'rep', 'tp')
- q_scale: float32 [2, 48, 6144], P(None, 'rep', 'tp')
- k_served: bfloat16 [2, 6144, 1024], P(None, 'rep', 'tp')
- k_scale: float32 [2, 48, 1024], P(None, 'rep', 'tp')
- v_served: bfloat16 [2, 6144, 1024], P(None, 'rep', 'tp')
- v_scale: float32 [2, 48, 1024], P(None, 'rep', 'tp')
- o_served: bfloat16 [2, 6144, 6144], P(None, 'tp', 'rep')
- o_scale: float32 [2, 48, 6144], P(None, 'tp', 'rep')
- gate_served: bfloat16 [2, 6144, 16384], P(None, 'rep', 'tp')
- gate_scale: float32 [2, 48, 16384], P(None, 'rep', 'tp')
- up_served: bfloat16 [2, 6144, 16384], P(None, 'rep', 'tp')
- up_scale: float32 [2, 48, 16384], P(None, 'rep', 'tp')
All inputs are finite; a program needn't handle non-finite values. Where the computation divides by a largest or mean magnitude, that divisor is 1e-20 or more.
Results may differ from a plain program's by a relative error of at most 0.001.
Values may be sent and summed in bfloat16 or wider, within the bound.
A program may use at most 192 MiB of HBM per device.

v0:
```python
import jax
import jax.numpy as jnp
from jax import lax
from jax.sharding import PartitionSpec as P

D = 6144
KV = 1024
FF = 16384
GROUP = 128
LAYERS = 2


def quantize(served):
    values = served.astype(jnp.float32)
    grouped = values.reshape(values.shape[0] // GROUP, GROUP, values.shape[1])
    peak = jnp.max(jnp.abs(grouped), axis=1) + 1e-06
    scaled = (grouped / peak[:, None, :]).astype(jnp.bfloat16)
    return (scaled.reshape(served.shape), peak)


def column_block(received):
    return received.reshape(-1, received.shape[3]).T


def output_block(received):
    return received.reshape(-1, received.shape[2]).T


def on_device(flat_buffer, shard_pad):
    devices = lax.axis_size("rep") * lax.axis_size("tp")
    widths = (D, KV, KV, D, FF, FF)
    columns = (0, 1, 2, 4, 5)
    tiled = flat_buffer.reshape(flat_buffer.shape[0] // 128, 128)
    offset = jnp.zeros((), jnp.int32)
    pieces = []
    for layer in range(LAYERS):
        layer_pieces = []
        for index in range(6):
            rows = widths[index] // devices
            lines = rows * D // 128
            taken = lax.dynamic_slice_in_dim(tiled, offset, lines, 0)
            layer_pieces.append(taken.reshape(rows, D))
            offset = offset + lines + shard_pad[layer, index]
        pieces.append(layer_pieces)
    blocks = [[None] * 6 for layer in range(LAYERS)]
    for layer in range(LAYERS):
        for index in columns:
            piece = pieces[layer][index]
            received = lax.all_to_all(
                lax.all_to_all(
                    piece.reshape(1, 1, piece.shape[0], D),
                    "rep",
                    split_axis=3,
                    concat_axis=0,
                    tiled=True,
                ),
                "tp",
                split_axis=0,
                concat_axis=1,
                tiled=True,
            )
            blocks[layer][index] = column_block(received)
        piece = pieces[layer][3]
        received_rows = lax.all_to_all(
            piece.reshape(1, piece.shape[0], D), "tp", split_axis=2, concat_axis=0, tiled=True
        )
        blocks[layer][3] = output_block(received_rows)
    results = []
    for index in range(6):
        scaled_list = []
        peak_list = []
        for layer in range(LAYERS):
            scaled, peak = quantize(blocks[layer][index])
            scaled_list.append(scaled)
            peak_list.append(peak)
        results.append(jnp.stack(scaled_list))
        results.append(jnp.stack(peak_list))
    return (
        results[0],
        results[1],
        results[2],
        results[3],
        results[4],
        results[5],
        results[6],
        results[7],
        results[8],
        results[9],
        results[10],
        results[11],
    )


def solution(mesh):
    return jax.shard_map(
        on_device,
        mesh=mesh,
        in_specs=(P(("rep", "tp")), P()),
        out_specs=(
            P(None, "rep", "tp"),
            P(None, "rep", "tp"),
            P(None, "rep", "tp"),
            P(None, "rep", "tp"),
            P(None, "rep", "tp"),
            P(None, "rep", "tp"),
            P(None, "tp", "rep"),
            P(None, "tp", "rep"),
            P(None, "rep", "tp"),
            P(None, "rep", "tp"),
            P(None, "rep", "tp"),
            P(None, "rep", "tp"),
        ),
        check_vma=False,
    )
```

profile of v0, /device:TPU:10, one launch (start us, length us, event | category | flops | bytes accessed | tf_op | source)
XLA Modules:
  0.0 1923.8 jit_solution(5891359268631695627)
XLA Ops:
  16.2 34.4 %reduce.2 = bf16[6144,32]{1,0:T(8,128)(2,1)} reduce(bf16[6144,1,1,32]{3,2,1,0:T(2,128)(2,1)S(1)} %bitcast.370, bf16[]{:T(256)} %broadcast.224), dimensions={1,2}, to_apply=%bitcast.303.reduce_sub_computation | reduce | bytes 786434
  66.9 34.4 %reduce.3 = bf16[6144,32]{1,0:T(8,128)(2,1)} reduce(bf16[6144,1,1,32]{3,2,1,0:T(2,128)(2,1)S(1)} %bitcast.371, bf16[]{:T(256)} %broadcast.224), dimensions={1,2}, to_apply=%bitcast.301.reduce_sub_computation | reduce | bytes 786434
  117.6 34.4 %reduce.4 = bf16[6144,32]{1,0:T(8,128)(2,1)} reduce(bf16[6144,1,1,32]{3,2,1,0:T(2,128)(2,1)S(1)} %bitcast.372, bf16[]{:T(256)} %broadcast.224), dimensions={1,2}, to_apply=%bitcast.307.reduce_sub_computation | reduce | bytes 786434
  165.6 34.4 %reduce.5 = bf16[6144,32]{1,0:T(8,128)(2,1)} reduce(bf16[6144,1,1,32]{3,2,1,0:T(2,128)(2,1)S(1)} %bitcast.373, bf16[]{:T(256)} %broadcast.224), dimensions={1,2}, to_apply=%bitcast.305.reduce_sub_computation | reduce | bytes 786434
  278.6 13.7 copy.337
  292.3 34.6 %reduce.1 = bf16[6144,192]{1,0:T(8,128)(2,1)S(1)} reduce(bf16[6144,1,1,192]{3,2,1,0:T(2,128)(2,1)} %bitcast.338, bf16[]{:T(256)} %broadcast.224), dimensions={1,2}, to_apply=%bitcast.297.reduce_sub_computation | reduce | bytes 4718594
  341.2 13.7 copy.330
  354.9 34.6 %reduce = bf16[6144,192]{1,0:T(8,128)(2,1)S(1)} reduce(bf16[6144,1,1,192]{3,2,1,0:T(2,128)(2,1)} %bitcast.339, bf16[]{:T(256)} %broadcast.224), dimensions={1,2}, to_apply=%bitcast.299.reduce_sub_computation | reduce | bytes 4718594
  402.0 13.7 copy.372
  415.7 34.6 %reduce.6 = bf16[6144,192]{1,0:T(8,128)(2,1)S(1)} reduce(bf16[6144,1,192]{2,1,0:T(2,128)(2,1)} %bitcast.340, bf16[]{:T(256)} %broadcast.224), dimensions={1}, to_apply=%bitcast.293.reduce_sub_computation | reduce | bytes 4718594
  462.4 13.7 copy.377
  476.1 34.6 %reduce.7 = bf16[6144,192]{1,0:T(8,128)(2,1)S(1)} reduce(bf16[6144,1,192]{2,1,0:T(2,128)(2,1)} %bitcast.341, bf16[]{:T(256)} %broadcast.224), dimensions={1}, to_apply=%bitcast.295.reduce_sub_computation | reduce | bytes 4718594
  522.0 19.1 constant_dynamic-slice_fusion.1
  551.2 26.5 %copy.394 = bf16[1,1,512,6144]{2,1,0,3:T(2,128)(2,1)} copy(bf16[1,1,512,6144]{3,2,1,0:T(8,128)(2,1)} %reshape_reshape.46) | data formatting | bytes 12582912 | tf_op jit(solution)/shard_map/reshape;reshape | solution.py:51
  577.7 41.6 %reduce.10 = bf16[6144,512]{1,0:T(8,128)(2,1)} reduce(bf16[6144,1,1,512]{3,2,1,0:T(2,128)(2,1)} %bitcast.330, bf16[]{:T(256)} %broadcast.224), dimensions={1,2}, to_apply=%bitcast.315.reduce_sub_computation | reduce | bytes 12582914
  645.0 26.5 %copy.400 = bf16[1,1,512,6144]{2,1,0,3:T(2,128)(2,1)} copy(bf16[1,1,512,6144]{3,2,1,0:T(8,128)(2,1)} %reshape_reshape.47) | data formatting | bytes 12582912 | tf_op jit(solution)/shard_map/reshape;reshape | solution.py:51
  671.5 41.7 %reduce.11 = bf16[6144,512]{1,0:T(8,128)(2,1)} reduce(bf16[6144,1,1,512]{3,2,1,0:T(2,128)(2,1)} %bitcast.331, bf16[]{:T(256)} %broadcast.224), dimensions={1,2}, to_apply=%bitcast.313.reduce_sub_computation | reduce | bytes 12582914
  737.7 26.5 %copy.382 = bf16[1,1,512,6144]{2,1,0,3:T(2,128)(2,1)} copy(bf16[1,1,512,6144]{3,2,1,0:T(8,128)(2,1)} %reshape_reshape.44) | data formatting | bytes 12582912 | tf_op jit(solution)/shard_map/reshape;reshape | solution.py:51
  764.2 41.7 %reduce.8 = bf16[6144,512]{1,0:T(8,128)(2,1)} reduce(bf16[6144,1,1,512]{3,2,1,0:T(2,128)(2,1)} %bitcast.332, bf16[]{:T(256)} %broadcast.224), dimensions={1,2}, to_apply=%bitcast.311.reduce_sub_computation | reduce | bytes 12582914
  830.0 26.5 %copy.388 = bf16[1,1,512,6144]{2,1,0,3:T(2,128)(2,1)} copy(bf16[1,1,512,6144]{3,2,1,0:T(8,128)(2,1)} %reshape_reshape.45) | data formatting | bytes 12582912 | tf_op jit(solution)/shard_map/reshape;reshape | solution.py:51
  856.6 41.7 %reduce.9 = bf16[6144,512]{1,0:T(8,128)(2,1)} reduce(bf16[6144,1,1,512]{3,2,1,0:T(2,128)(2,1)} %bitcast.329, bf16[]{:T(256)} %broadcast.224), dimensions={1,2}, to_apply=%bitcast.309.reduce_sub_computation | reduce | bytes 12582914
  920.7 14.0 copy.338
  937.2 45.3 %all-to-all-done.16 = bf16[8,2,196608]{2,1,0:T(2,128)(2,1)} async-done(((bf16[8,2,196608]{2,1,0:T(2,128)(2,1)}), bf16[8,2,196608]{2,1,0:T(2,128)(2,1)}, u32[]{:S(2)}, u32[]{:S(2)}) %all-to-all-start.16) | async-done | bytes 6291488 | tf_op jit(solution)/shard_map/all_to_all | solution.py:50
  996.2 13.3 copy.331
  1013.6 25.0 %all-to-all-done.3 = bf16[8,1,192,768]{3,2,1,0:T(8,128)(2,1)S(1)} async-done(((bf16[8,1,192,768]{3,2,1,0:T(8,128)(2,1)}), bf16[8,1,192,768]{3,2,1,0:T(8,128)(2,1)S(1)}, u32[]{:S(2)}, u32[]{:S(2)}) %all-to-all-start.3) | async-done | bytes 2359328 | tf_op jit(solution)/shard_map/all_to_all | solution.py:49
  1046.4 11.0 reshape.408
  1066.5 30.0 %all-to-all-done.1 = bf16[8,1,192,768]{3,2,1,0:T(8,128)(2,1)} async-done(((bf16[8,1,192,768]{3,2,1,0:T(8,128)(2,1)}), bf16[8,1,192,768]{3,2,1,0:T(8,128)(2,1)}, u32[]{:S(2)}, u32[]{:S(2)}) %all-to-all-start.1) | async-done | bytes 2359328 | tf_op jit(solution)/shard_map/all_to_all | solution.py:49
  1105.1 11.0 reshape.406
  1125.2 114.3 %all-to-all-done.19 = bf16[8,1,512,768]{2,3,1,0:T(8,128)(2,1)} async-done(((bf16[8,1,512,768]{2,3,1,0:T(8,128)(2,1)}), bf16[8,1,512,768]{2,3,1,0:T(8,128)(2,1)}, u32[]{:S(2)}, u32[]{:S(2)}) %all-to-all-start.19) | async-done | bytes 6291488 | tf_op jit(solution)/shard_map/all_to_all | solution.py:49
  1301.2 13.3 copy.373
  1345.5 13.3 copy.378
  1391.6 11.0 reshape.404
  1446.2 11.0 reshape.402
  1559.4 10.4 bitcast_abs_fusion.1
  1569.8 12.7 copy.398
  1620.7 10.4 bitcast_abs_fusion
  1631.1 12.7 copy.404
  1656.3 12.7 copy.399
  1675.3 12.6 copy.405
  1711.1 16.6 copy.416
  1755.1 10.4 bitcast_abs_fusion.3
  1765.5 12.9 copy.386
  1811.1 10.4 bitcast_abs_fusion.2
  1821.6 12.7 copy.392
  1846.1 12.7 copy.387
  1858.8 12.0 fusion.3
  1877.1 12.7 copy.393
  1905.1 16.6 copy.414
  (262 shorter events, 789.7 us)
Async XLA Ops:
  54.4 50.7 %all-to-all-start.4 = ((bf16[8,2,12288]{2,1,0:T(2,128)(2,1)}), bf16[8,2,12288]{2,1,0:T(2,128)(2,1)S(1)}, u32[]{:S(2)}, u32[]{:S(2)}) async-start(bf16[8,2,12288]{2,1,0:T(2,128)(2,1)} %reshape.395), calls=%async_computation.4 | async-start | bytes 786432 | tf_op jit(solution)/shard_map/all_to_all | solution.py:50
  105.1 50.7 %copy-start.12 = (bf16[8,2,12288]{2,1,0:T(2,128)(2,1)}, bf16[8,2,12288]{2,1,0:T(2,128)(2,1)S(1)}, u32[]{:S(2)}) copy-start(bf16[8,2,12288]{2,1,0:T(2,128)(2,1)S(1)} %all-to-all-done.4) | copy-start | bytes 1179652
  105.1 50.7 %all-to-all-start.6 = ((bf16[8,2,12288]{2,1,0:T(2,128)(2,1)}), bf16[8,2,12288]{2,1,0:T(2,128)(2,1)}, u32[]{:S(2)}, u32[]{:S(2)}) async-start(bf16[8,2,12288]{2,1,0:T(2,128)(2,1)} %reshape.393), calls=%async_computation.6 | async-start | bytes 786432 | tf_op jit(solution)/shard_map/all_to_all | solution.py:50
  155.8 48.0 %all-to-all-start.8 = ((bf16[8,2,12288]{2,1,0:T(2,128)(2,1)}), bf16[8,2,12288]{2,1,0:T(2,128)(2,1)}, u32[]{:S(2)}, u32[]{:S(2)}) async-start(bf16[8,2,12288]{2,1,0:T(2,128)(2,1)} %reshape.399), calls=%async_computation.8 | async-start | bytes 786432 | tf_op jit(solution)/shard_map/all_to_all | solution.py:50
  203.8 15.1 all-to-all-start.10
  218.9 16.2 all-to-all-start.5
  235.1 16.2 all-to-all-start.7
  251.3 13.4 all-to-all-start.9
  264.7 67.4 %all-to-all-start.11 = ((bf16[8,1,32,768]{3,2,1,0:T(8,128)(2,1)}), bf16[8,1,32,768]{3,2,1,0:T(8,128)(2,1)S(1)}, u32[]{:S(2)}, u32[]{:S(2)}) async-start(bf16[8,1,32,768]{3,2,1,0:T(8,128)(2,1)} %copy.367), calls=%async_computation.11 | async-start | bytes 786432 | tf_op jit(solution)/shard_map/all_to_all | solution.py:49
  332.1 9.1 copy-start.13
  332.1 62.6 %all-to-all-start.2 = ((bf16[8,2,73728]{2,1,0:T(2,128)(2,1)}), bf16[8,2,73728]{2,1,0:T(2,128)(2,1)}, u32[]{:S(2)}, u32[]{:S(2)}) async-start(bf16[8,2,73728]{2,1,0:T(2,128)(2,1)} %reshape.389), calls=%async_computation.2 | async-start | bytes 4718592 | tf_op jit(solution)/shard_map/all_to_all | solution.py:50
  394.7 4.8 copy-start.8
  394.7 60.0 %all-to-all-start = ((bf16[8,2,73728]{2,1,0:T(2,128)(2,1)}), bf16[8,2,73728]{2,1,0:T(2,128)(2,1)}, u32[]{:S(2)}, u32[]{:S(2)}) async-start(bf16[8,2,73728]{2,1,0:T(2,128)(2,1)} %reshape.391), calls=%async_computation | async-start | bytes 4718592 | tf_op jit(solution)/shard_map/all_to_all | solution.py:50
  454.8 5.2 copy-start.7
  454.8 60.4 %all-to-all-start.12 = ((bf16[4,2,147456]{2,1,0:T(2,128)(2,1)}), bf16[4,2,147456]{2,1,0:T(2,128)(2,1)}, u32[]{:S(2)}, u32[]{:S(2)}) async-start(bf16[4,2,147456]{2,1,0:T(2,128)(2,1)} %reshape.385), calls=%async_computation.12 | async-start | bytes 4718592 | tf_op jit(solution)/shard_map/all_to_all | solution.py:64
  515.2 113.6 %all-to-all-start.13 = ((bf16[4,2,147456]{2,1,0:T(2,128)(2,1)}), bf16[4,2,147456]{2,1,0:T(2,128)(2,1)S(1)}, u32[]{:S(2)}, u32[]{:S(2)}) async-start(bf16[4,2,147456]{2,1,0:T(2,128)(2,1)} %reshape.387), calls=%async_computation.13 | async-start | bytes 4718592 | tf_op jit(solution)/shard_map/all_to_all | solution.py:64
  628.8 1.5 copy-start.6
  630.3 92.3 %all-to-all-start.18 = ((bf16[8,2,196608]{2,1,0:T(2,128)(2,1)}), bf16[8,2,196608]{2,1,0:T(2,128)(2,1)}, u32[]{:S(2)}, u32[]{:S(2)}) async-start(bf16[8,2,196608]{2,1,0:T(2,128)(2,1)} %reshape.407), calls=%async_computation.18 | async-start | bytes 12582912 | tf_op jit(solution)/shard_map/all_to_all | solution.py:50
  722.6 92.7 %all-to-all-start.20 = ((bf16[8,2,196608]{2,1,0:T(2,128)(2,1)}), bf16[8,2,196608]{2,1,0:T(2,128)(2,1)}, u32[]{:S(2)}, u32[]{:S(2)}) async-start(bf16[8,2,196608]{2,1,0:T(2,128)(2,1)} %reshape.405), calls=%async_computation.20 | async-start | bytes 12582912 | tf_op jit(solution)/shard_map/all_to_all | solution.py:50
  815.3 92.3 %all-to-all-start.14 = ((bf16[8,2,196608]{2,1,0:T(2,128)(2,1)}), bf16[8,2,196608]{2,1,0:T(2,128)(2,1)}, u32[]{:S(2)}, u32[]{:S(2)}) async-start(bf16[8,2,196608]{2,1,0:T(2,128)(2,1)} %reshape.403), calls=%async_computation.14 | async-start | bytes 12582912 | tf_op jit(solution)/shard_map/all_to_all | solution.py:50
  907.6 74.9 %all-to-all-start.16 = ((bf16[8,2,196608]{2,1,0:T(2,128)(2,1)}), bf16[8,2,196608]{2,1,0:T(2,128)(2,1)}, u32[]{:S(2)}, u32[]{:S(2)}) async-start(bf16[8,2,196608]{2,1,0:T(2,128)(2,1)} %reshape.401), calls=%async_computation.16 | async-start | bytes 12582912 | tf_op jit(solution)/shard_map/all_to_all | solution.py:50
  982.6 56.1 %all-to-all-start.3 = ((bf16[8,1,192,768]{3,2,1,0:T(8,128)(2,1)}), bf16[8,1,192,768]{3,2,1,0:T(8,128)(2,1)S(1)}, u32[]{:S(2)}, u32[]{:S(2)}) async-start(bf16[8,1,192,768]{3,2,1,0:T(8,128)(2,1)} %copy.339), calls=%async_computation.3 | async-start | bytes 4718592 | tf_op jit(solution)/shard_map/all_to_all | solution.py:49
  1038.6 57.9 %all-to-all-start.1 = ((bf16[8,1,192,768]{3,2,1,0:T(8,128)(2,1)}), bf16[8,1,192,768]{3,2,1,0:T(8,128)(2,1)}, u32[]{:S(2)}, u32[]{:S(2)}) async-start(bf16[8,1,192,768]{3,2,1,0:T(8,128)(2,1)} %copy.332), calls=%async_computation.1 | async-start | bytes 4718592 | tf_op jit(solution)/shard_map/all_to_all | solution.py:49
  1096.5 142.9 %all-to-all-start.19 = ((bf16[8,1,512,768]{2,3,1,0:T(8,128)(2,1)}), bf16[8,1,512,768]{2,3,1,0:T(8,128)(2,1)}, u32[]{:S(2)}, u32[]{:S(2)}) async-start(bf16[8,1,512,768]{2,3,1,0:T(8,128)(2,1)} %bitcast.345), calls=%async_computation.19 | async-start | bytes 12582912 | tf_op jit(solution)/shard_map/all_to_all | solution.py:49
  1239.4 172.2 %all-to-all-start.21 = ((bf16[8,1,512,768]{2,3,1,0:T(8,128)(2,1)}), bf16[8,1,512,768]{2,3,1,0:T(8,128)(2,1)}, u32[]{:S(2)}, u32[]{:S(2)}) async-start(bf16[8,1,512,768]{2,3,1,0:T(8,128)(2,1)} %bitcast.342), calls=%async_computation.21 | async-start | bytes 12582912 | tf_op jit(solution)/shard_map/all_to_all | solution.py:49
  1254.0 0.9 copy-start.10
  1268.8 8.3 copy-start.14
  1277.2 0.9 copy-start.11
  1281.4 11.6 copy-start.17
  1324.8 2.1 copy-start.1
  1369.2 2.2 copy-start.3
  1411.6 185.0 %all-to-all-start.15 = ((bf16[8,1,512,768]{2,3,1,0:T(8,128)(2,1)}), bf16[8,1,512,768]{2,3,1,0:T(8,128)(2,1)}, u32[]{:S(2)}, u32[]{:S(2)}) async-start(bf16[8,1,512,768]{2,3,1,0:T(8,128)(2,1)} %bitcast.344), calls=%async_computation.15 | async-start | bytes 12582912 | tf_op jit(solution)/shard_map/all_to_all | solution.py:49
  1431.5 4.8 copy-start.9
  1467.0 2.2 copy-start.2
  1483.0 2.2 copy-start.4
  1508.9 11.1 slice-start
  1515.4 5.0 slice-start.1
  1515.4 6.4 copy-start.5
  1596.6 187.3 %all-to-all-start.17 = ((bf16[8,1,512,768]{2,3,1,0:T(8,128)(2,1)}), bf16[8,1,512,768]{2,3,1,0:T(8,128)(2,1)}, u32[]{:S(2)}, u32[]{:S(2)}) async-start(bf16[8,1,512,768]{2,3,1,0:T(8,128)(2,1)} %bitcast.343), calls=%async_computation.17 | async-start | bytes 12582912 | tf_op jit(solution)/shard_map/all_to_all | solution.py:49
  1687.9 11.9 copy-start
  1877.1 22.1 %slice-start.2 = ((s8[6291456]{0:T(1024)(128)(4,1)}), s8[2097152]{0:T(1024)(128)(4,1)S(1)}, s32[]{:S(2)}) async-start(s8[6291456]{0:T(1024)(128)(4,1)} %bitcast.354), calls=%async_computation.24 | async-start | bytes 4194304
  1889.8 9.5 slice-start.3
  1905.1 17.5 copy-start.15
  1905.1 17.5 copy-start.16
where the time goes:
time: 1950 us; the launch traced here: 1920 us
  local copies, waits for them, and re-layouts  923 us (47%)
  other arithmetic  653 us (33%)
  waiting for transfers between devices  217 us (11%)
  starting transfers between devices  120 us (6%)
    unnamed x14, other arithmetic  443 us
    unnamed x91, local copies, waits for them, and re-layouts  274 us
    another operation x20, local copies, waits for them, and re-layouts, on_device(): piece.reshape(1, 1, piece.shape[0], D)  204 us
    all_to_all x10, waiting for transfers between devices, on_device(): lax.all_to_all(lax.all_to_all(piece.reshape(1, 1, piece.shape[0], D), 're...  171 us
    div x24, local copies, waits for them, and re-layouts, quantize(): scaled = (grouped / peak[:, None, :]).astype(jnp.bfloat16)  124 us
    abs x12, local copies, waits for them, and re-layouts, quantize(): peak = jnp.max(jnp.abs(grouped), axis=1) + 1e-06  84.2 us
    all_to_all x10, starting transfers between devices, on_device(): lax.all_to_all(lax.all_to_all(piece.reshape(1, 1, piece.shape[0], D), 're...  63.1 us
    convert_element_type x14, local copies, waits for them, and re-layouts, quantize(): values = served.astype(jnp.float32)  61.9 us
  transfers between devices with their start and end apart: 22, of which 5 were waited for; matrix products, arithmetic and copies ran while one was open for 71% of the time, Pallas kernels for 0%

commit v1 on v0

--- a/solution.py
+++ b/solution.py
@@ -46,18 +46,26 @@
     for layer in range(LAYERS):
         for index in columns:
             piece = pieces[layer][index]
-            received = lax.all_to_all(
+            received = jnp.concatenate(
                 lax.all_to_all(
-                    piece.reshape(1, 1, piece.shape[0], D),
-                    "rep",
-                    split_axis=3,
-                    concat_axis=0,
-                    tiled=True,
+                    jnp.stack(
+                        jnp.split(
+                            lax.all_to_all(
+                                piece.reshape(1, 1, piece.shape[0], D),
+                                "rep",
+                                split_axis=3,
+                                concat_axis=0,
+                                tiled=True,
+                            ),
+                            lax.axis_size("tp"),
+                            axis=0,
+                        )
+                    ),
+                    "tp",
+                    0,
+                    0,
                 ),
-                "tp",
-                split_axis=0,
-                concat_axis=1,
-                tiled=True,
+                axis=1,
             )
             blocks[layer][index] = column_block(received)
         piece = pieces[layer][3]

time: 1950 us -> 1920 us (0.985)
  local copies, waits for them, and re-layouts: 923 us -> 882 us
  other arithmetic: 653 us -> 673 us
    all_to_all x4 -> x0, local copies, waits for them, and re-layouts: 34.5 us -> none  [on_device(): lax.all_to_all(lax.all_to_all(piece.reshape(1, 1, piece.shape[0], D), 're...]
    another operation x0 -> x10, other arithmetic: none -> 30.3 us  [on_device(): jnp.stack(jnp.split(lax.all_to_all(piece.reshape(1, 1, piece.shape[0], D)...]
    all_to_all x12 -> x6, local copies, waits for them, and re-layouts: 51.5 us -> 44.6 us  [on_device(): lax.all_to_all(piece.reshape(1, 1, piece.shape[0], D), 'rep', split_axis=...]
    unnamed x91 -> x99, local copies, waits for them, and re-layouts: 274 us -> 270 us
    unnamed x14 -> x16, other arithmetic: 443 us -> 443 us
  transfers between devices with their start and end apart: 22 -> 22, of which waited for: 5 -> 6; matrix products, arithmetic and copies ran while one was open for 71% -> 72% of each run, Pallas kernels for 0% -> 0%
where the time goes in v1:
time: 1920 us; the launch traced here: 1890 us
  local copies, waits for them, and re-layouts  882 us (46%)
  other arithmetic  673 us (35%)
  waiting for transfers between devices  208 us (11%)
  starting transfers between devices  120 us (6%)
    unnamed x16, other arithmetic  443 us
    unnamed x99, local copies, waits for them, and re-layouts  270 us
    another operation x20, local copies, waits for them, and re-layouts, on_device(): piece.reshape(1, 1, piece.shape[0], D)  207 us
    all_to_all x10, waiting for transfers between devices, on_device(): lax.all_to_all(jnp.stack(jnp.split(lax.all_to_all(piece.reshape(1, 1, pie...  163 us
    div x24, local copies, waits for them, and re-layouts, quantize(): scaled = (grouped / peak[:, None, :]).astype(jnp.bfloat16)  114 us
    abs x12, local copies, waits for them, and re-layouts, quantize(): peak = jnp.max(jnp.abs(grouped), axis=1) + 1e-06  77.1 us
    convert_element_type x14, local copies, waits for them, and re-layouts, quantize(): values = served.astype(jnp.float32)  69.7 us
    all_to_all x10, starting transfers between devices, on_device(): lax.all_to_all(jnp.stack(jnp.split(lax.all_to_all(piece.reshape(1, 1, pie...  62.6 us
  transfers between devices with their start and end apart: 22, of which 6 were waited for; matrix products, arithmetic and copies ran while one was open for 72% of the time, Pallas kernels for 0%

profile of v1, /device:TPU:10, one launch (start us, length us, event | category | flops | bytes accessed | tf_op | source)
XLA Modules:
  0.0 1892.9 jit_solution(1142161302370312318)
XLA Ops:
  16.2 34.4 %reduce.4 = bf16[6144,32]{1,0:T(8,128)(2,1)} reduce(bf16[6144,1,1,32]{3,2,1,0:T(2,128)(2,1)S(1)} %bitcast.390, bf16[]{:T(256)} %broadcast.224), dimensions={1,2}, to_apply=%bitcast.327.reduce_sub_computation | reduce | bytes 786434
  67.0 34.4 %reduce.5 = bf16[6144,32]{1,0:T(8,128)(2,1)} reduce(bf16[6144,1,1,32]{3,2,1,0:T(2,128)(2,1)S(1)} %bitcast.391, bf16[]{:T(256)} %broadcast.224), dimensions={1,2}, to_apply=%bitcast.325.reduce_sub_computation | reduce | bytes 786434
  118.7 34.4 %reduce.2 = bf16[6144,32]{1,0:T(8,128)(2,1)} reduce(bf16[6144,1,1,32]{3,2,1,0:T(2,128)(2,1)S(1)} %bitcast.392, bf16[]{:T(256)} %broadcast.224), dimensions={1,2}, to_apply=%bitcast.323.reduce_sub_computation | reduce | bytes 786434
  170.1 34.4 %reduce.3 = bf16[6144,32]{1,0:T(8,128)(2,1)} reduce(bf16[6144,1,1,32]{3,2,1,0:T(2,128)(2,1)S(1)} %bitcast.393, bf16[]{:T(256)} %broadcast.224), dimensions={1,2}, to_apply=%bitcast.321.reduce_sub_computation | reduce | bytes 786434
  291.7 13.7 copy.411
  305.4 34.6 %reduce.1 = bf16[6144,192]{1,0:T(8,128)(2,1)S(1)} reduce(bf16[6144,1,1,192]{3,2,1,0:T(2,128)(2,1)} %bitcast.360, bf16[]{:T(256)} %broadcast.224), dimensions={1,2}, to_apply=%bitcast.317.reduce_sub_computation | reduce | bytes 4718594
  354.2 13.7 copy.404
  367.9 34.6 %reduce = bf16[6144,192]{1,0:T(8,128)(2,1)S(1)} reduce(bf16[6144,1,1,192]{3,2,1,0:T(2,128)(2,1)} %bitcast.361, bf16[]{:T(256)} %broadcast.224), dimensions={1,2}, to_apply=%bitcast.319.reduce_sub_computation | reduce | bytes 4718594
  414.6 13.7 copy.446
  428.3 34.6 %reduce.6 = bf16[6144,192]{1,0:T(8,128)(2,1)S(1)} reduce(bf16[6144,1,192]{2,1,0:T(2,128)(2,1)} %bitcast.362, bf16[]{:T(256)} %broadcast.224), dimensions={1}, to_apply=%bitcast.313.reduce_sub_computation | reduce | bytes 4718594
  475.3 13.7 copy.451
  489.0 34.6 %reduce.7 = bf16[6144,192]{1,0:T(8,128)(2,1)S(1)} reduce(bf16[6144,1,192]{2,1,0:T(2,128)(2,1)} %bitcast.363, bf16[]{:T(256)} %broadcast.224), dimensions={1}, to_apply=%bitcast.315.reduce_sub_computation | reduce | bytes 4718594
  534.4 19.1 %constant_dynamic-slice_fusion.1 = (bf16[24576,128]{1,0:T(8,128)(2,1)}, bf16[24576,128]{1,0:T(8,128)(2,1)}, bf16[24576,128]{1,0:T(8,128)(2,1)}, bf16[24576,128]{1,0:T(8,128)(2,1)}) fusion(bf16[141336,128]{1,0:T(8,128)(2,1)} %bitcast.359, s32[]{:T(128)S(6)} %select_n.42, s32[]{:T(128)S(6)} %select_n.43, s32[]{:T(128)S(6)} %select_n.41, s32[]{:T(128)S(6)} %select_n.40), kind=kLoop, calls=%fused_computation.121 | loop fusion | bytes 50331664 | tf_op jit(solution)/shard_map/dynamic_slice | solution.py:41
  563.6 26.5 %copy.468 = bf16[1,1,512,6144]{2,1,0,3:T(2,128)(2,1)} copy(bf16[1,1,512,6144]{3,2,1,0:T(8,128)(2,1)} %reshape_reshape.56) | data formatting | bytes 12582912 | tf_op jit(solution)/shard_map/reshape;reshape | solution.py:54
  590.1 41.6 %reduce.10 = bf16[6144,512]{1,0:T(8,128)(2,1)} reduce(bf16[6144,1,1,512]{3,2,1,0:T(2,128)(2,1)} %bitcast.350, bf16[]{:T(256)} %broadcast.224), dimensions={1,2}, to_apply=%bitcast.335.reduce_sub_computation | reduce | bytes 12582914
  657.7 26.5 %copy.474 = bf16[1,1,512,6144]{2,1,0,3:T(2,128)(2,1)} copy(bf16[1,1,512,6144]{3,2,1,0:T(8,128)(2,1)} %reshape_reshape.57) | data formatting | bytes 12582912 | tf_op jit(solution)/shard_map/reshape;reshape | solution.py:54
  684.3 41.7 %reduce.11 = bf16[6144,512]{1,0:T(8,128)(2,1)} reduce(bf16[6144,1,1,512]{3,2,1,0:T(2,128)(2,1)} %bitcast.351, bf16[]{:T(256)} %broadcast.224), dimensions={1,2}, to_apply=%bitcast.333.reduce_sub_computation | reduce | bytes 12582914
  750.1 26.5 %copy.456 = bf16[1,1,512,6144]{2,1,0,3:T(2,128)(2,1)} copy(bf16[1,1,512,6144]{3,2,1,0:T(8,128)(2,1)} %reshape_reshape.54) | data formatting | bytes 12582912 | tf_op jit(solution)/shard_map/reshape;reshape | solution.py:54
  776.6 41.7 %reduce.8 = bf16[6144,512]{1,0:T(8,128)(2,1)} reduce(bf16[6144,1,1,512]{3,2,1,0:T(2,128)(2,1)} %bitcast.352, bf16[]{:T(256)} %broadcast.224), dimensions={1,2}, to_apply=%bitcast.331.reduce_sub_computation | reduce | bytes 12582914
  843.0 26.5 %copy.462 = bf16[1,1,512,6144]{2,1,0,3:T(2,128)(2,1)} copy(bf16[1,1,512,6144]{3,2,1,0:T(8,128)(2,1)} %reshape_reshape.55) | data formatting | bytes 12582912 | tf_op jit(solution)/shard_map/reshape;reshape | solution.py:54
  869.6 41.7 %reduce.9 = bf16[6144,512]{1,0:T(8,128)(2,1)} reduce(bf16[6144,1,1,512]{3,2,1,0:T(2,128)(2,1)} %bitcast.349, bf16[]{:T(256)} %broadcast.224), dimensions={1,2}, to_apply=%bitcast.329.reduce_sub_computation | reduce | bytes 12582914
  933.7 14.0 copy.412
  955.9 39.6 %all-to-all-done.16 = bf16[8,2,196608]{2,1,0:T(2,128)(2,1)} async-done(((bf16[8,2,196608]{2,1,0:T(2,128)(2,1)}), bf16[8,2,196608]{2,1,0:T(2,128)(2,1)}, u32[]{:S(2)}, u32[]{:S(2)}) %all-to-all-start.16) | async-done | bytes 6291488 | tf_op jit(solution)/shard_map/all_to_all | solution.py:53
  1008.9 13.3 copy.405
  1032.1 19.3 %all-to-all-done.3 = bf16[4,2,1,192,768]{4,1,3,2,0:T(2,128)(2,1)S(1)} async-done(((bf16[4,2,1,192,768]{4,1,3,2,0:T(2,128)(2,1)}), bf16[4,2,1,192,768]{4,1,3,2,0:T(2,128)(2,1)S(1)}, u32[]{:S(2)}, u32[]{:S(2)}) %all-to-all-start.3) | async-done | bytes 2359328 | tf_op jit(solution)/shard_map/all_to_all | solution.py:50
  1059.4 11.0 reshape.448
  1080.4 29.1 %all-to-all-done.1 = bf16[4,2,1,192,768]{4,1,3,2,0:T(2,128)(2,1)} async-done(((bf16[4,2,1,192,768]{4,1,3,2,0:T(2,128)(2,1)}), bf16[4,2,1,192,768]{4,1,3,2,0:T(2,128)(2,1)}, u32[]{:S(2)}, u32[]{:S(2)}) %all-to-all-start.1) | async-done | bytes 2359328 | tf_op jit(solution)/shard_map/all_to_all | solution.py:50
  1118.0 11.0 reshape.446
  1139.1 113.3 %all-to-all-done.19 = bf16[4,2,1,512,768]{3,4,1,2,0:T(8,128)(2,1)} async-done(((bf16[4,2,1,512,768]{3,4,1,2,0:T(8,128)(2,1)}), bf16[4,2,1,512,768]{3,4,1,2,0:T(8,128)(2,1)}, u32[]{:S(2)}, u32[]{:S(2)}) %all-to-all-start.19) | async-done | bytes 6291488 | tf_op jit(solution)/shard_map/all_to_all | solution.py:50
  1285.9 14.0 copy.447
  1328.2 14.0 copy.452
  1399.6 11.0 reshape.444
  1419.7 11.3 reshape.442
  1533.0 12.6 copy.471
  1556.0 12.7 copy.472
  1583.5 12.6 copy.477
  1611.7 12.7 copy.478
  1637.1 12.7 copy.473
  1656.1 12.7 copy.479
  1692.0 16.6 copy.490
  1717.9 12.6 copy.459
  1740.9 12.7 copy.460
  1768.4 12.8 copy.465
  1791.6 12.8 copy.466
  1817.1 12.7 copy.461
  1829.7 12.0 fusion.3
  1848.0 12.8 copy.467
  1876.1 16.6 copy.488
  (282 shorter events, 761.6 us)
Async XLA Ops:
  54.4 50.8 %all-to-all-start.8 = ((bf16[8,2,12288]{2,1,0:T(2,128)(2,1)}), bf16[8,2,12288]{2,1,0:T(2,128)(2,1)S(1)}, u32[]{:S(2)}, u32[]{:S(2)}) async-start(bf16[8,2,12288]{2,1,0:T(2,128)(2,1)} %reshape.439), calls=%async_computation.8 | async-start | bytes 786432 | tf_op jit(solution)/shard_map/all_to_all | solution.py:53
  105.2 0.7 copy-start.15
  105.9 51.0 %all-to-all-start.10 = ((bf16[8,2,12288]{2,1,0:T(2,128)(2,1)}), bf16[8,2,12288]{2,1,0:T(2,128)(2,1)S(1)}, u32[]{:S(2)}, u32[]{:S(2)}) async-start(bf16[8,2,12288]{2,1,0:T(2,128)(2,1)} %reshape.437), calls=%async_computation.10 | async-start | bytes 786432 | tf_op jit(solution)/shard_map/all_to_all | solution.py:53
  156.9 0.7 copy-start.14
  157.6 60.7 %all-to-all-start.4 = ((bf16[8,2,12288]{2,1,0:T(2,128)(2,1)}), bf16[8,2,12288]{2,1,0:T(2,128)(2,1)S(1)}, u32[]{:S(2)}, u32[]{:S(2)}) async-start(bf16[8,2,12288]{2,1,0:T(2,128)(2,1)} %reshape.435), calls=%async_computation.4 | async-start | bytes 786432 | tf_op jit(solution)/shard_map/all_to_all | solution.py:53
  218.4 0.7 copy-start.13
  219.1 11.0 all-to-all-start.6
  230.2 17.2 all-to-all-start.9
  247.3 17.2 all-to-all-start.11
  264.5 13.5 all-to-all-start.5
  278.0 67.2 %all-to-all-start.7 = ((bf16[4,2,1,32,768]{4,1,3,2,0:T(2,128)(2,1)}), bf16[4,2,1,32,768]{4,1,3,2,0:T(2,128)(2,1)S(1)}, u32[]{:S(2)}, u32[]{:S(2)}) async-start(bf16[4,2,1,32,768]{4,1,3,2,0:T(2,128)(2,1)} %pad_maximum_fusion.13), calls=%async_computation.7 | async-start | bytes 786432 | tf_op jit(solution)/shard_map/all_to_all | solution.py:50
  345.3 6.5 copy-start.16
  345.3 62.4 %all-to-all-start.2 = ((bf16[8,2,73728]{2,1,0:T(2,128)(2,1)}), bf16[8,2,73728]{2,1,0:T(2,128)(2,1)}, u32[]{:S(2)}, u32[]{:S(2)}) async-start(bf16[8,2,73728]{2,1,0:T(2,128)(2,1)} %reshape.429), calls=%async_computation.2 | async-start | bytes 4718592 | tf_op jit(solution)/shard_map/all_to_all | solution.py:53
  407.7 4.5 copy-start.12
  407.7 59.7 %all-to-all-start = ((bf16[8,2,73728]{2,1,0:T(2,128)(2,1)}), bf16[8,2,73728]{2,1,0:T(2,128)(2,1)}, u32[]{:S(2)}, u32[]{:S(2)}) async-start(bf16[8,2,73728]{2,1,0:T(2,128)(2,1)} %reshape.431), calls=%async_computation | async-start | bytes 4718592 | tf_op jit(solution)/shard_map/all_to_all | solution.py:53
  467.4 5.4 copy-start.11
  467.4 60.7 %all-to-all-start.12 = ((bf16[4,2,147456]{2,1,0:T(2,128)(2,1)}), bf16[4,2,147456]{2,1,0:T(2,128)(2,1)}, u32[]{:S(2)}, u32[]{:S(2)}) async-start(bf16[4,2,147456]{2,1,0:T(2,128)(2,1)} %reshape.425), calls=%async_computation.12 | async-start | bytes 4718592 | tf_op jit(solution)/shard_map/all_to_all | solution.py:72
  528.1 113.2 %all-to-all-start.13 = ((bf16[4,2,147456]{2,1,0:T(2,128)(2,1)}), bf16[4,2,147456]{2,1,0:T(2,128)(2,1)S(1)}, u32[]{:S(2)}, u32[]{:S(2)}) async-start(bf16[4,2,147456]{2,1,0:T(2,128)(2,1)} %reshape.427), calls=%async_computation.13 | async-start | bytes 4718592 | tf_op jit(solution)/shard_map/all_to_all | solution.py:72
  641.2 1.4 copy-start.9
  642.7 92.6 %all-to-all-start.18 = ((bf16[8,2,196608]{2,1,0:T(2,128)(2,1)}), bf16[8,2,196608]{2,1,0:T(2,128)(2,1)}, u32[]{:S(2)}, u32[]{:S(2)}) async-start(bf16[8,2,196608]{2,1,0:T(2,128)(2,1)} %reshape.447), calls=%async_computation.18 | async-start | bytes 12582912 | tf_op jit(solution)/shard_map/all_to_all | solution.py:53
  735.3 92.5 %all-to-all-start.20 = ((bf16[8,2,196608]{2,1,0:T(2,128)(2,1)}), bf16[8,2,196608]{2,1,0:T(2,128)(2,1)}, u32[]{:S(2)}, u32[]{:S(2)}) async-start(bf16[8,2,196608]{2,1,0:T(2,128)(2,1)} %reshape.445), calls=%async_computation.20 | async-start | bytes 12582912 | tf_op jit(solution)/shard_map/all_to_all | solution.py:53
  827.8 92.9 %all-to-all-start.14 = ((bf16[8,2,196608]{2,1,0:T(2,128)(2,1)}), bf16[8,2,196608]{2,1,0:T(2,128)(2,1)}, u32[]{:S(2)}, u32[]{:S(2)}) async-start(bf16[8,2,196608]{2,1,0:T(2,128)(2,1)} %reshape.443), calls=%async_computation.14 | async-start | bytes 12582912 | tf_op jit(solution)/shard_map/all_to_all | solution.py:53
  920.7 74.9 %all-to-all-start.16 = ((bf16[8,2,196608]{2,1,0:T(2,128)(2,1)}), bf16[8,2,196608]{2,1,0:T(2,128)(2,1)}, u32[]{:S(2)}, u32[]{:S(2)}) async-start(bf16[8,2,196608]{2,1,0:T(2,128)(2,1)} %reshape.441), calls=%async_computation.16 | async-start | bytes 12582912 | tf_op jit(solution)/shard_map/all_to_all | solution.py:53
  995.6 55.9 %all-to-all-start.3 = ((bf16[4,2,1,192,768]{4,1,3,2,0:T(2,128)(2,1)}), bf16[4,2,1,192,768]{4,1,3,2,0:T(2,128)(2,1)S(1)}, u32[]{:S(2)}, u32[]{:S(2)}) async-start(bf16[4,2,1,192,768]{4,1,3,2,0:T(2,128)(2,1)} %pad_maximum_fusion.9), calls=%async_computation.3 | async-start | bytes 4718592 | tf_op jit(solution)/shard_map/all_to_all | solution.py:50
  1051.4 18.9 copy-start.7
  1051.4 58.0 %all-to-all-start.1 = ((bf16[4,2,1,192,768]{4,1,3,2,0:T(2,128)(2,1)}), bf16[4,2,1,192,768]{4,1,3,2,0:T(2,128)(2,1)}, u32[]{:S(2)}, u32[]{:S(2)}) async-start(bf16[4,2,1,192,768]{4,1,3,2,0:T(2,128)(2,1)} %pad_maximum_fusion.8), calls=%async_computation.1 | async-start | bytes 4718592 | tf_op jit(solution)/shard_map/all_to_all | solution.py:50
  1109.4 143.0 %all-to-all-start.19 = ((bf16[4,2,1,512,768]{3,4,1,2,0:T(8,128)(2,1)}), bf16[4,2,1,512,768]{3,4,1,2,0:T(8,128)(2,1)}, u32[]{:S(2)}, u32[]{:S(2)}) async-start(bf16[4,2,1,512,768]{3,4,1,2,0:T(8,128)(2,1)} %pad_maximum_fusion.4), calls=%async_computation.19 | async-start | bytes 12582912 | tf_op jit(solution)/shard_map/all_to_all | solution.py:50
  1252.4 191.4 %all-to-all-start.21 = ((bf16[4,2,1,512,768]{3,4,1,2,0:T(8,128)(2,1)}), bf16[4,2,1,512,768]{3,4,1,2,0:T(8,128)(2,1)}, u32[]{:S(2)}, u32[]{:S(2)}) async-start(bf16[4,2,1,512,768]{3,4,1,2,0:T(8,128)(2,1)} %pad_maximum_fusion.5), calls=%async_computation.21 | async-start | bytes 12582912 | tf_op jit(solution)/shard_map/all_to_all | solution.py:50
  1269.7 3.6 copy-start.17
  1308.6 2.1 copy-start.2
  1319.6 3.1 copy-start.10
  1351.4 2.2 copy-start.4
  1376.3 10.9 slice-start.2
  1382.4 4.9 slice-start.3
  1382.4 6.4 copy-start.5
  1419.7 20.5 %slice-start.4 = ((s8[6291456]{0:T(1024)(128)(4,1)}), s8[2097152]{0:T(1024)(128)(4,1)S(1)}, s32[]{:S(2)}) async-start(s8[6291456]{0:T(1024)(128)(4,1)} %bitcast.365), calls=%async_computation.26 | async-start | bytes 4194304
  1431.0 9.3 slice-start.5
  1443.8 152.3 %all-to-all-start.15 = ((bf16[4,2,1,512,768]{3,4,1,2,0:T(8,128)(2,1)}), bf16[4,2,1,512,768]{3,4,1,2,0:T(8,128)(2,1)}, u32[]{:S(2)}, u32[]{:S(2)}) async-start(bf16[4,2,1,512,768]{3,4,1,2,0:T(8,128)(2,1)} %pad_maximum_fusion.2), calls=%async_computation.15 | async-start | bytes 12582912 | tf_op jit(solution)/shard_map/all_to_all | solution.py:50
  1452.3 3.2 copy-start.8
  1457.6 2.2 copy-start.1
  1474.9 2.2 copy-start.3
  1500.8 10.7 slice-start
  1506.9 4.9 slice-start.1
  1506.9 6.4 copy-start.6
  1596.1 162.9 %all-to-all-start.17 = ((bf16[4,2,1,512,768]{3,4,1,2,0:T(8,128)(2,1)}), bf16[4,2,1,512,768]{3,4,1,2,0:T(8,128)(2,1)}, u32[]{:S(2)}, u32[]{:S(2)}) async-start(bf16[4,2,1,512,768]{3,4,1,2,0:T(8,128)(2,1)} %pad_maximum_fusion.3), calls=%async_computation.17 | async-start | bytes 12582912 | tf_op jit(solution)/shard_map/all_to_all | solution.py:50
  1668.7 11.9 copy-start
  1848.0 22.1 %slice-start.6 = ((s8[6291456]{0:T(1024)(128)(4,1)}), s8[2097152]{0:T(1024)(128)(4,1)S(1)}, s32[]{:S(2)}) async-start(s8[6291456]{0:T(1024)(128)(4,1)} %bitcast.374), calls=%async_computation.28 | async-start | bytes 4194304
  1860.8 9.5 slice-start.7
